TPU v7x, 32 devices: a whole 2x2x4 slice. The times are simulated.
32 devices in a mesh: dp: 8 (over z, y), mp: 4 (over x, core).
Axes of the slice: x: 2, y: 2, z: 4, core: 2. Of those that a mesh axis runs over, the one named last changes fastest.
Arguments:
- image_tokens: bfloat16 [8, 192, 3072], P('dp'), may hold values from -6 to 6
- text_tokens: bfloat16 [8, 64, 3072], P('dp'), may hold values from -6 to 6
- null_prompt: bfloat16 [64, 3072], replicated, may hold values from -6 to 6
- drop_flags: int32 [8], P('dp'), may hold values 0 or 1
- time_index: int32 [8], P('dp'), may hold values from 0 to 31
- modulation: float32 [32, 3, 3072], replicated, may hold values from -3 to 3
- w_up: bfloat16 [3072, 12288], P('dp', 'mp'), may hold values from -0.109375 to 0.109375
- w_down: bfloat16 [12288, 3072], P('mp', 'dp'), may hold values from -0.0546875 to 0.0546875
- d_output: bfloat16 [8, 256, 3072], P('dp'), may hold values from -6 to 6
Outputs:
- block_out: bfloat16 [8, 256, 3072], P('dp')
- d_tokens: bfloat16 [8, 256, 3072], P('dp')
- grad_up: float32 [3072, 12288], P('dp', 'mp')
- grad_down: float32 [12288, 3072], P('mp', 'dp')
- grad_null: float32 [64, 3072], replicated
All inputs are finite; a program needn't handle non-finite values. No bound on the sum of `drop_flags` on one device may be relied on, other than what follows from the above.
Results may differ from a plain program's by a relative error of at most 0.017.
Values may be sent and summed in bfloat16 or wider, within the bound.
A program may use at most 128 MiB of HBM per device.

v0:
```python
import functools
import jax
import jax.numpy as jnp
from jax import lax
from jax.sharding import PartitionSpec as P

EPS = 1e-06
BF16 = jnp.bfloat16
F32 = jnp.float32


def gelu_tanh(values):
    return jax.nn.gelu(values, approximate=True)


def dot(left, right, dims):
    return lax.dot_general(left, right, (dims, ((), ())), preferred_element_type=F32)


def swap(values, axis, size, bit):
    return lax.ppermute(values, axis, [(i, i ^ bit) for i in range(size)])


def shards(
    dp,
    mp,
    image_tokens,
    text_tokens,
    null_prompt,
    drop_flags,
    time_index,
    modulation,
    w_up,
    w_down,
    d_output,
):
    lines = [list(range(parity, dp, 2)) for parity in range(2)]
    per_line = dp // 2
    bits = []
    bit = 1
    while bit < mp:
        bits.append(bit)
        bit *= 2
    d_rows, ff_m = w_up.shape
    f = ff_m // dp
    width = d_rows * dp
    up_own = lax.all_to_all(
        w_up.reshape(d_rows, dp, f).transpose(1, 0, 2), "dp", 0, 0, tiled=True
    ).reshape(width, f)
    down_own = (
        lax.all_to_all(w_down.reshape(dp, f, d_rows), "dp", 0, 0, tiled=True)
        .transpose(1, 0, 2)
        .reshape(f, width)
    )
    up_other = swap(up_own, "dp", dp, 1)
    down_other = swap(down_own, "dp", dp, 1)
    m = lax.axis_index("mp")
    n_text = text_tokens.shape[1] // mp
    n_image = image_tokens.shape[1] // mp
    all_text = text_tokens.shape[1]

    def share(text_part, image_part):
        t = lax.dynamic_slice_in_dim(text_part, m * n_text, n_text, 0)
        i = lax.dynamic_slice_in_dim(image_part, m * n_image, n_image, 0)
        return jnp.concatenate([t, i], axis=0)

    dropped = drop_flags[0] == 1
    joined32 = share(jnp.where(dropped, null_prompt, text_tokens[0]), image_tokens[0]).astype(F32)
    d_out32 = share(d_output[0, :all_text], d_output[0, all_text:]).astype(F32)
    level = lax.dynamic_index_in_dim(modulation, time_index[0], 0, keepdims=False)
    shift, scale, gate = (level[0][None], level[1][None], level[2][None])
    centred = joined32 - jnp.mean(joined32, axis=-1, keepdims=True)
    inv_std = lax.rsqrt(jnp.mean(centred * centred, axis=-1, keepdims=True) + EPS)
    normed = centred * inv_std
    mod_in = (normed * (1.0 + scale) + shift).astype(BF16)
    d_branch = (d_out32 * gate).astype(BF16)

    def gather(rows):
        rows = lax.all_gather(rows, "dp", axis=0, tiled=True, axis_index_groups=lines)
        for b in reversed(bits):
            rows = jnp.concatenate([rows, swap(rows, "mp", mp, b)], axis=0)
        return rows

    def scatter(own, other, block_own, block_other, contract):

        def product(rows):
            return dot(own[rows], block_own, contract) + dot(other[rows], block_other, contract)

        half = own.shape[0] // 2
        sent = swap(product(slice(half, None)).astype(BF16), "mp", mp, bits[0])
        total = product(slice(0, half)) + sent.astype(F32)
        for b in bits[1:]:
            half = total.shape[0] // 2
            total = total[:half] + swap(total[half:].astype(BF16), "mp", mp, b).astype(F32)
        parts = lax.all_to_all(
            total.astype(BF16).reshape(per_line, -1, width),
            "dp",
            0,
            0,
            tiled=True,
            axis_index_groups=lines,
        )
        return jnp.sum(parts.astype(F32), axis=0)

    tokens = gather(mod_in)
    d_tok = gather(d_branch)

    def half_block(up, down):
        pre = dot(tokens, up, ((1,), (0,)))
        hid, back = jax.vjp(gelu_tanh, pre)
        d_hid = dot(d_tok, down, ((1,), (1,)))
        return (hid.astype(BF16), back(d_hid)[0].astype(BF16))

    hid_own, dpre_own = half_block(up_own, down_own)
    hid_other, dpre_other = half_block(up_other, down_other)
    branch = scatter(hid_own, hid_other, down_own, down_other, ((1,), (0,)))
    d_mod = scatter(dpre_own, dpre_other, up_own, up_other, ((1,), (1,)))
    up_sent = dot(tokens, dpre_other, ((0,), (0,))).astype(BF16)
    down_sent = dot(hid_other, d_tok, ((0,), (0,))).astype(BF16)
    up_back = swap(up_sent, "dp", dp, 1)
    down_back = swap(down_sent, "dp", dp, 1)
    g_up = dot(tokens, dpre_own, ((0,), (0,))) + up_back.astype(F32)
    g_down = dot(hid_own, d_tok, ((0,), (0,))) + down_back.astype(F32)
    grad_up = (
        lax.all_to_all(g_up.astype(BF16).reshape(dp, d_rows, f), "dp", 0, 0, tiled=True)
        .transpose(1, 0, 2)
        .reshape(d_rows, ff_m)
        .astype(F32)
    )
    grad_down = (
        lax.all_to_all(
            g_down.astype(BF16).reshape(f, dp, d_rows).transpose(1, 0, 2), "dp", 0, 0, tiled=True
        )
        .reshape(ff_m, d_rows)
        .astype(F32)
    )
    block_out = (joined32 + gate * branch).astype(BF16)
    d_normed = d_mod * (1.0 + scale)
    d_full = d_out32 + inv_std * (
        d_normed
        - jnp.mean(d_normed, axis=-1, keepdims=True)
        - normed * jnp.mean(d_normed * normed, axis=-1, keepdims=True)
    )
    null_part = jnp.where(dropped, d_full[:n_text], F32(0.0)).astype(BF16)
    null_sum = lax.psum(null_part, "dp")

    def whole(rows):
        every = lax.all_gather(rows, "mp", axis=0)
        return jnp.concatenate(
            [every[:, :n_text].reshape(-1, width), every[:, n_text:].reshape(-1, width)], axis=0
        )[None]

    grad_null = lax.all_gather(null_sum, "mp", axis=0, tiled=True).astype(F32)
    return (whole(block_out), whole(d_full.astype(BF16)), grad_up, grad_down, grad_null)


def solution(mesh):
    placed = (
        P("dp", None, None),
        P("dp", None, None),
        P(),
        P("dp"),
        P("dp"),
        P(),
        P("dp", "mp"),
        P("mp", "dp"),
        P("dp", None, None),
    )
    return jax.shard_map(
        functools.partial(shards, mesh.shape["dp"], mesh.shape["mp"]),
        mesh=mesh,
        in_specs=placed,
        out_specs=(P("dp", None, None), P("dp", None, None), P("dp", "mp"), P("mp", "dp"), P()),
        check_vma=False,
    )
```

profile of v0, /device:TPU:0, one launch (start us, length us, event | category | flops | bytes accessed | tf_op | source)
XLA Modules:
  0.0 627.2 jit_solution(12918581351889117631)
XLA Ops:
  13.5 7.3 %all-to-all-start.1 = ((bf16[8,384,384]{2,1,0:T(8,128)(2,1)}), bf16[8,384,384]{2,1,0:T(8,128)(2,1)S(1)}, u32[]{:S(2)}, u32[]{:S(2)}) async-start(bf16[8,384,384]{2,1,0:T(8,128)(2,1)} %bitcast.115), calls=%async_computation.1 | async-start | bytes 4718592 | tf_op jit(solution)/shard_map/all_to_all | solution.py:51
  22.8 68.6 %all-gather.5.cloned.1.call-done = bf16[256,3072]{1,0:T(8,128)(2,1)} async-done(((bf16[64,3072]{1,0:T(8,128)(2,1)}), bf16[256,3072]{1,0:T(8,128)(2,1)}) %all-gather.5.cloned.1.call-update) | async-done | bytes 1572880 | tf_op jit(solution)/shard_map/all_gather | solution.py:79
  92.9 35.0 %all-gather.9.cloned.1.call-done = bf16[256,3072]{1,0:T(8,128)(2,1)} async-done(((bf16[64,3072]{1,0:T(8,128)(2,1)}), bf16[256,3072]{1,0:T(8,128)(2,1)}) %all-gather.9.cloned.1.call-update) | async-done | bytes 1572880 | tf_op jit(solution)/shard_map/all_gather | solution.py:79
  143.4 20.1 %collective-permute-done.6 = bf16[256,3072]{1,0:T(8,128)(2,1)} collective-permute-done((bf16[256,3072]{1,0:T(8,128)(2,1)}, bf16[256,3072]{1,0:T(8,128)(2,1)}, u32[]{:S(2)}, u32[]{:S(2)}) %collective-permute-start.6) | collective-permute-done | bytes 1572896 | tf_op jit(solution)/shard_map/ppermute | solution.py:21
  180.6 11.9 %all-to-all-done = bf16[8,384,384]{1,2,0:T(8,128)(2,1)} async-done(((bf16[8,384,384]{1,2,0:T(8,128)(2,1)}), bf16[8,384,384]{1,2,0:T(8,128)(2,1)}, u32[]{:S(2)}, u32[]{:S(2)}) %all-to-all-start) | async-done | bytes 2359328 | tf_op jit(solution)/shard_map/all_to_all | solution.py:47
  211.5 17.3 %collective-permute-done.3 = bf16[384,3072]{0,1:T(8,128)(2,1)} collective-permute-done((bf16[384,3072]{0,1:T(8,128)(2,1)S(1)}, bf16[384,3072]{0,1:T(8,128)(2,1)}, u32[]{:S(2)}, u32[]{:S(2)}) %collective-permute-start.3) | collective-permute-done | bytes 2359328 | tf_op jit(solution)/shard_map/ppermute | solution.py:21
  228.8 6.2 fusion.47
  239.4 39.6 %collective-permute-done.2 = bf16[3072,384]{1,0:T(8,128)(2,1)S(1)} collective-permute-done((bf16[3072,384]{1,0:T(8,128)(2,1)}, bf16[3072,384]{1,0:T(8,128)(2,1)S(1)}, u32[]{:S(2)}, u32[]{:S(2)}) %collective-permute-start.2) | collective-permute-done | bytes 2359328 | tf_op jit(solution)/shard_map/ppermute | solution.py:21
  311.8 29.3 %collective-permute-done.10 = bf16[3072,384]{1,0:T(8,128)(2,1)S(1)} collective-permute-done((bf16[3072,384]{1,0:T(8,128)(2,1)S(1)}, bf16[3072,384]{1,0:T(8,128)(2,1)S(1)}, u32[]{:S(2)}, u32[]{:S(2)}) %collective-permute-start.10) | collective-permute-done | bytes 2359328 | tf_op jit(solution)/shard_map/ppermute | solution.py:21
  345.9 6.9 %all-to-all-start.4 = ((bf16[8,384,384]{2,1,0:T(8,128)(2,1)}), bf16[8,384,384]{2,1,0:T(8,128)(2,1)}, u32[]{:S(2)}, u32[]{:S(2)}) async-start(bf16[8,384,384]{2,1,0:T(8,128)(2,1)} %bitcast.116), calls=%async_computation.4 | async-start | bytes 4718592 | tf_op jit(solution)/shard_map/all_to_all | solution.py:125
  352.8 6.3 %fusion.30 = f32[512,3072]{1,0:T(8,128)} fusion(bf16[3072,384]{1,0:T(8,128)(2,1)} %copy-done.2, bf16[1024,384]{1,0:T(8,128)(2,1)S(1)} %copy-done.15), kind=kOutput, calls=%fused_computation.66 | convolution fusion | flops 1207959552 | bytes 9043968 | tf_op jit(solution)/shard_map/dot_general | solution.py:17
  359.2 8.1 %convert_add_fusion = f32[512,3072]{1,0:T(8,128)} fusion(bf16[512,3072]{1,0:T(8,128)(2,1)} %collective-permute-done.8, f32[512,3072]{1,0:T(8,128)S(1)} %bitcast.86, f32[512,3072]{1,0:T(8,128)} %fusion.30), kind=kLoop, calls=%fused_computation | loop fusion | flops 4718592 | bytes 22020096 | tf_op jit(solution)/shard_map/add | solution.py:91
  375.9 6.8 %convert_add_fusion.1 = f32[512,3072]{1,0:T(8,128)} fusion(bf16[512,3072]{1,0:T(8,128)(2,1)} %collective-permute-done.4, f32[512,3072]{1,0:T(8,128)S(1)} %bitcast.84, f32[512,3072]{1,0:T(8,128)S(1)} %fusion.37), kind=kLoop, calls=%fused_computation.2 | loop fusion | flops 4718592 | bytes 22020096 | tf_op jit(solution)/shard_map/add | solution.py:91
  386.5 21.8 %collective-permute-done.9 = bf16[256,3072]{1,0:T(8,128)(2,1)} collective-permute-done((bf16[256,3072]{1,0:T(8,128)(2,1)}, bf16[256,3072]{1,0:T(8,128)(2,1)}, u32[]{:S(2)}, u32[]{:S(2)}) %collective-permute-start.9) | collective-permute-done | bytes 1572896 | tf_op jit(solution)/shard_map/ppermute | solution.py:21
  417.5 7.2 %convolution_convert_fusion = bf16[384,3072]{1,0:T(8,128)(2,1)} fusion(bf16[1024,384]{1,0:T(8,128)(2,1)} %copy-done.13, bf16[1024,3072]{1,0:T(8,128)(2,1)} %constant_dynamic-update-slice_fusion.3), kind=kOutput, calls=%fused_computation.7 | convolution fusion | flops 2417098752 | bytes 9437184 | tf_op jit(solution)/shard_map/dot_general | solution.py:17
  428.1 11.5 %collective-permute-done.5 = bf16[256,3072]{1,0:T(8,128)(2,1)} collective-permute-done((bf16[256,3072]{1,0:T(8,128)(2,1)}, bf16[256,3072]{1,0:T(8,128)(2,1)}, u32[]{:S(2)}, u32[]{:S(2)}) %collective-permute-start.5) | collective-permute-done | bytes 1572896 | tf_op jit(solution)/shard_map/ppermute | solution.py:21
  442.6 6.9 %all-to-all-done.3 = bf16[4,64,3072]{2,1,0:T(8,128)(2,1)} async-done(((bf16[4,64,3072]{2,1,0:T(8,128)(2,1)}), bf16[4,64,3072]{2,1,0:T(8,128)(2,1)}, u32[]{:S(2)}, u32[]{:S(2)}) %all-to-all-start.3) | async-done | bytes 1572896 | tf_op jit(solution)/shard_map/all_to_all | solution.py:95
  453.3 19.4 %collective-permute-done.11 = bf16[384,3072]{1,0:T(8,128)(2,1)} collective-permute-done((bf16[384,3072]{1,0:T(8,128)(2,1)}, bf16[384,3072]{1,0:T(8,128)(2,1)}, u32[]{:S(2)}, u32[]{:S(2)}) %collective-permute-start.11) | collective-permute-done | bytes 2359328 | tf_op jit(solution)/shard_map/ppermute | solution.py:21
  472.7 6.1 add_convert_fusion.2
  501.5 46.0 %all-to-all-done.5 = bf16[8,384,384]{2,1,0:T(8,128)(2,1)S(1)} async-done(((bf16[8,384,384]{2,1,0:T(8,128)(2,1)}), bf16[8,384,384]{2,1,0:T(8,128)(2,1)S(1)}, u32[]{:S(2)}, u32[]{:S(2)}) %all-to-all-start.5) | async-done | bytes 2359328 | tf_op jit(solution)/shard_map/all_to_all | solution.py:131
  550.3 25.2 %all-reduce.2.cloned.1.call-done = bf16[16,3072]{1,0:T(8,128)(2,1)} async-done(((bf16[16,3072]{1,0:T(8,128)(2,1)}), bf16[16,3072]{1,0:T(8,128)(2,1)}) %all-reduce.2.cloned.1.call-update) | async-done | bytes 98320 | tf_op jit(solution)/shard_map/psum | solution.py:145
  575.5 6.6 %all_gather.21 = bf16[64,3072]{1,0:T(8,128)(2,1)S(1)} all-gather(bf16[16,3072]{1,0:T(8,128)(2,1)} %all-reduce.2.cloned.1.call-done), channel_id=1, replica_groups=mesh['dp'=8,'mp'=4] {'mp'}, dimensions={0}, use_global_device_ids=true | all-gather | bytes 491520 | tf_op jit(solution)/shard_map/all_gather | solution.py:153
  583.0 13.1 %all-gather.7.cloned.1.call-done = bf16[4,64,3072]{2,1,0:T(8,128)(2,1)} async-done(((bf16[1,64,3072]{2,1,0:T(8,128)(2,1)}), bf16[4,64,3072]{2,1,0:T(8,128)(2,1)}) %all-gather.7.cloned.1.call-update) | async-done | bytes 1572880 | tf_op jit(solution)/shard_map/all_gather | solution.py:148
  598.8 19.0 %all-gather.11.cloned.1.call-done = bf16[4,64,3072]{2,1,0:T(8,128)(2,1)} async-done(((bf16[1,64,3072]{2,1,0:T(8,128)(2,1)}), bf16[4,64,3072]{2,1,0:T(8,128)(2,1)}) %all-gather.11.cloned.1.call-update) | async-done | bytes 1572880 | tf_op jit(solution)/shard_map/all_gather | solution.py:148
  (166 shorter events, 165.0 us)
Async XLA Ops:
  7.2 84.3 %all-gather.5.cloned.1.call-start = ((), (), s32[]{:S(2)}) async-start(), calls=%async_computation.6 | async-start | bytes 1966080 | tf_op jit(solution)/shard_map/all_gather | solution.py:79
  13.5 120.1 %all-to-all-start.1 = ((bf16[8,384,384]{2,1,0:T(8,128)(2,1)}), bf16[8,384,384]{2,1,0:T(8,128)(2,1)S(1)}, u32[]{:S(2)}, u32[]{:S(2)}) async-start(bf16[8,384,384]{2,1,0:T(8,128)(2,1)} %bitcast.115), calls=%async_computation.1 | async-start | bytes 4718592 | tf_op jit(solution)/shard_map/all_to_all | solution.py:51
  20.9 107.0 %all-gather.9.cloned.1.call-start = ((), (), s32[]{:S(2)}) async-start(), calls=%async_computation.8 | async-start | bytes 1966080 | tf_op jit(solution)/shard_map/all_gather | solution.py:79
  21.9 111.7 %copy-start.12 = (bf16[1,64,3072]{2,1,0:T(8,128)(2,1)}, bf16[1,64,3072]{2,1,0:T(8,128)(2,1)S(1)}, u32[]{:S(2)}) copy-start(bf16[1,64,3072]{2,1,0:T(8,128)(2,1)S(1)} %slice.82) | copy-start | bytes 1179652
  91.4 48.0 %collective-permute-start = (bf16[256,3072]{1,0:T(8,128)(2,1)}, bf16[256,3072]{1,0:T(8,128)(2,1)}, u32[]{:S(2)}, u32[]{:S(2)}) collective-permute-start(bf16[256,3072]{1,0:T(8,128)(2,1)} %all-gather.5.cloned.1.call-done), channel_id=1, source_target_pairs={{0,2},{1,3},{2,0},{3,1},{4,6},{5,7},{6,4},{7,5},{8,10},{9,11},{10,... | collective-permute-start | bytes 4718600 | tf_op jit(solution)/shard_map/ppermute | solution.py:21
  127.9 35.6 %collective-permute-start.6 = (bf16[256,3072]{1,0:T(8,128)(2,1)}, bf16[256,3072]{1,0:T(8,128)(2,1)}, u32[]{:S(2)}, u32[]{:S(2)}) collective-permute-start(bf16[256,3072]{1,0:T(8,128)(2,1)} %all-gather.9.cloned.1.call-done), channel_id=1, source_target_pairs={{0,2},{1,3},{2,0},{3,1},{4,6},{5,7},{6,4},{7,5},{8,10},{9,11},{10,... | collective-permute-start | bytes 4718600 | tf_op jit(solution)/shard_map/ppermute | solution.py:21
  135.1 57.4 %all-to-all-start = ((bf16[8,384,384]{1,2,0:T(8,128)(2,1)}), bf16[8,384,384]{1,2,0:T(8,128)(2,1)}, u32[]{:S(2)}, u32[]{:S(2)}) async-start(bf16[8,384,384]{1,2,0:T(8,128)(2,1)} %bitcast.103), calls=%async_computation | async-start | bytes 4718592 | tf_op jit(solution)/shard_map/all_to_all | solution.py:47
  143.4 54.9 %collective-permute-start.1 = (bf16[512,3072]{1,0:T(8,128)(2,1)}, bf16[512,3072]{1,0:T(8,128)(2,1)}, u32[]{:S(2)}, u32[]{:S(2)}) collective-permute-start(bf16[512,3072]{1,0:T(8,128)(2,1)} %pad_maximum_fusion), channel_id=1, source_target_pairs={{0,1},{1,0},{2,3},{3,2},{4,5},{5,4},{6,7},{7,6},{8,9},{9,8},{10,11... | collective-permute-start | bytes 9437192 | tf_op jit(solution)/shard_map/ppermute | solution.py:21
  166.7 35.3 %collective-permute-start.7 = (bf16[512,3072]{1,0:T(8,128)(2,1)}, bf16[512,3072]{1,0:T(8,128)(2,1)}, u32[]{:S(2)}, u32[]{:S(2)}) collective-permute-start(bf16[512,3072]{1,0:T(8,128)(2,1)} %pad_maximum_fusion.1), channel_id=1, source_target_pairs={{0,1},{1,0},{2,3},{3,2},{4,5},{5,4},{6,7},{7,6},{8,9},{9,8},{10,11... | collective-permute-start | bytes 9437192 | tf_op jit(solution)/shard_map/ppermute | solution.py:21
  171.0 57.8 %collective-permute-start.3 = (bf16[384,3072]{0,1:T(8,128)(2,1)S(1)}, bf16[384,3072]{0,1:T(8,128)(2,1)}, u32[]{:S(2)}, u32[]{:S(2)}) collective-permute-start(bf16[384,3072]{0,1:T(8,128)(2,1)S(1)} %bitcast.87), channel_id=1, source_target_pairs={{0,4},{4,0},{8,12},{12,8},{16,20},{20,16},{24,28},{28,24},{1,5},{5... | collective-permute-start | bytes 7077896 | tf_op jit(solution)/shard_map/ppermute | solution.py:21
  196.8 82.3 %collective-permute-start.2 = (bf16[3072,384]{1,0:T(8,128)(2,1)}, bf16[3072,384]{1,0:T(8,128)(2,1)S(1)}, u32[]{:S(2)}, u32[]{:S(2)}) collective-permute-start(bf16[3072,384]{1,0:T(8,128)(2,1)} %bitcast.91), channel_id=1, source_target_pairs={{0,4},{4,0},{8,12},{12,8},{16,20},{20,16},{24,28},{28,24},{1,5},{5... | collective-permute-start | bytes 7077896 | tf_op jit(solution)/shard_map/ppermute | solution.py:21
  287.6 53.5 %collective-permute-start.10 = (bf16[3072,384]{1,0:T(8,128)(2,1)S(1)}, bf16[3072,384]{1,0:T(8,128)(2,1)S(1)}, u32[]{:S(2)}, u32[]{:S(2)}) collective-permute-start(bf16[3072,384]{1,0:T(8,128)(2,1)S(1)} %convolution_convert_fusion.1), channel_id=1, source_target_pairs={{0,4},{4,0},{8,12},{12,8},{16,20},{20,16},{24,28},{28,24},{1,5},{5... | collective-permute-start | bytes 7077896 | tf_op jit(solution)/shard_map/ppermute | solution.py:21
  295.4 63.8 %collective-permute-start.8 = (bf16[512,3072]{1,0:T(8,128)(2,1)}, bf16[512,3072]{1,0:T(8,128)(2,1)}, u32[]{:S(2)}, u32[]{:S(2)}) collective-permute-start(bf16[512,3072]{1,0:T(8,128)(2,1)} %add_convert_fusion), channel_id=1, source_target_pairs={{0,1},{1,0},{2,3},{3,2},{4,5},{5,4},{6,7},{7,6},{8,9},{9,8},{10,11... | collective-permute-start | bytes 9437192 | tf_op jit(solution)/shard_map/ppermute | solution.py:21
  302.5 73.4 %collective-permute-start.4 = (bf16[512,3072]{1,0:T(8,128)(2,1)}, bf16[512,3072]{1,0:T(8,128)(2,1)}, u32[]{:S(2)}, u32[]{:S(2)}) collective-permute-start(bf16[512,3072]{1,0:T(8,128)(2,1)} %add_convert_fusion.1), channel_id=1, source_target_pairs={{0,1},{1,0},{2,3},{3,2},{4,5},{5,4},{6,7},{7,6},{8,9},{9,8},{10,11... | collective-permute-start | bytes 9437192 | tf_op jit(solution)/shard_map/ppermute | solution.py:21
  345.9 66.3 %all-to-all-start.4 = ((bf16[8,384,384]{2,1,0:T(8,128)(2,1)}), bf16[8,384,384]{2,1,0:T(8,128)(2,1)}, u32[]{:S(2)}, u32[]{:S(2)}) async-start(bf16[8,384,384]{2,1,0:T(8,128)(2,1)} %bitcast.116), calls=%async_computation.4 | async-start | bytes 4718592 | tf_op jit(solution)/shard_map/all_to_all | solution.py:125
  370.7 37.6 %collective-permute-start.9 = (bf16[256,3072]{1,0:T(8,128)(2,1)}, bf16[256,3072]{1,0:T(8,128)(2,1)}, u32[]{:S(2)}, u32[]{:S(2)}) collective-permute-start(bf16[256,3072]{1,0:T(8,128)(2,1)} %slice.154), channel_id=1, source_target_pairs={{0,2},{1,3},{2,0},{3,1},{4,6},{5,7},{6,4},{7,5},{8,10},{9,11},{10,... | collective-permute-start | bytes 4718600 | tf_op jit(solution)/shard_map/ppermute | solution.py:21
  385.9 53.6 %collective-permute-start.5 = (bf16[256,3072]{1,0:T(8,128)(2,1)}, bf16[256,3072]{1,0:T(8,128)(2,1)}, u32[]{:S(2)}, u32[]{:S(2)}) collective-permute-start(bf16[256,3072]{1,0:T(8,128)(2,1)} %slice.155), channel_id=1, source_target_pairs={{0,2},{1,3},{2,0},{3,1},{4,6},{5,7},{6,4},{7,5},{8,10},{9,11},{10,... | collective-permute-start | bytes 4718600 | tf_op jit(solution)/shard_map/ppermute | solution.py:21
  412.3 37.2 %all-to-all-start.3 = ((bf16[4,64,3072]{2,1,0:T(8,128)(2,1)}), bf16[4,64,3072]{2,1,0:T(8,128)(2,1)}, u32[]{:S(2)}, u32[]{:S(2)}) async-start(bf16[4,64,3072]{2,1,0:T(8,128)(2,1)} %bitcast.106), calls=%async_computation.3 | async-start | bytes 3145728 | tf_op jit(solution)/shard_map/all_to_all | solution.py:95
  424.7 48.0 %collective-permute-start.11 = (bf16[384,3072]{1,0:T(8,128)(2,1)}, bf16[384,3072]{1,0:T(8,128)(2,1)}, u32[]{:S(2)}, u32[]{:S(2)}) collective-permute-start(bf16[384,3072]{1,0:T(8,128)(2,1)} %convolution_convert_fusion), channel_id=1, source_target_pairs={{0,4},{4,0},{8,12},{12,8},{16,20},{20,16},{24,28},{28,24},{1,5},{5... | collective-permute-start | bytes 7077896 | tf_op jit(solution)/shard_map/ppermute | solution.py:21
  449.4 38.7 %all-to-all-start.2 = ((bf16[4,64,3072]{2,1,0:T(8,128)(2,1)}), bf16[4,64,3072]{2,1,0:T(8,128)(2,1)S(1)}, u32[]{:S(2)}, u32[]{:S(2)}) async-start(bf16[4,64,3072]{2,1,0:T(8,128)(2,1)} %bitcast.105), calls=%async_computation.2 | async-start | bytes 3145728 | tf_op jit(solution)/shard_map/all_to_all | solution.py:95
  453.0 122.5 %all-reduce.2.cloned.1.call-start = ((), (), s32[]{:S(2)}) async-start(), calls=%async_computation.10 | async-start | bytes 196608 | tf_op jit(solution)/shard_map/psum | solution.py:145
  489.3 58.2 %all-to-all-start.5 = ((bf16[8,384,384]{2,1,0:T(8,128)(2,1)}), bf16[8,384,384]{2,1,0:T(8,128)(2,1)S(1)}, u32[]{:S(2)}, u32[]{:S(2)}) async-start(bf16[8,384,384]{2,1,0:T(8,128)(2,1)} %bitcast.101), calls=%async_computation.5 | async-start | bytes 4718592 | tf_op jit(solution)/shard_map/all_to_all | solution.py:131
  492.9 103.2 %all-gather.7.cloned.1.call-start = ((), (), s32[]{:S(2)}) async-start(), calls=%async_computation.7 | async-start | bytes 1966080 | tf_op jit(solution)/shard_map/all_gather | solution.py:148
  496.1 121.7 %all-gather.11.cloned.1.call-start = ((), (), s32[]{:S(2)}) async-start(), calls=%async_computation.9 | async-start | bytes 1966080 | tf_op jit(solution)/shard_map/all_gather | solution.py:148
  (36 other events, 410.8 us)
Sparse Core Ops, SparseCore 0:
  13.6 77.7 all-gather.4
  93.6 34.2 all-gather.8
  485.4 90.0 all-reduce.1
  577.5 18.6 all-gather.6
  598.1 19.6 all-gather.10
where the time goes:
time: 638 us; the launch traced here: 627 us
  waiting for transfers between devices  388 us (61%)
  matrix products  74.1 us (12%)
  other arithmetic  49.7 us (8%)
  local copies, waits for them, and re-layouts  49 us (8%)
  starting transfers between devices  43.8 us (7%)
  between operations  15.9 us (2%)
  blocking collectives  6.63 us (1%)
    ppermute x12, waiting for transfers between devices, swap(): return lax.ppermute(values, axis, [(i, i ^ bit) for i in range(size)])  159 us
    all_gather x2, waiting for transfers between devices, gather(): lax.all_gather(rows, 'dp', axis=0, tiled=True, axis_index_groups=lines)  104 us
    dot_general x16, matrix products, dot(): lax.dot_general(left, right, (dims, ((), ())), preferred_element_type=F32)  74.1 us
    all_to_all x1, waiting for transfers between devices, shards(): lax.all_to_all(g_down.astype(BF16).reshape(f, dp, d_rows).transpose(1, 0,...  46 us
    all_gather x2, waiting for transfers between devices, whole(): every = lax.all_gather(rows, 'mp', axis=0)  32.1 us
    psum x1, waiting for transfers between devices, shards(): null_sum = lax.psum(null_part, 'dp')  25.2 us
    unnamed x69, local copies, waits for them, and re-layouts  17.3 us
    add x2, other arithmetic, scatter(): total = product(slice(0, half)) + sent.astype(F32)  14.9 us
  transfers between devices with their start and end apart: 23, of which 16 were waited for; matrix products, arithmetic and copies ran while one was open for 24% of the time, Pallas kernels for 0%

commit v1 on v0

--- a/solution.py
+++ b/solution.py
@@ -142,7 +142,7 @@
         - normed * jnp.mean(d_normed * normed, axis=-1, keepdims=True)
     )
     null_part = jnp.where(dropped, d_full[:n_text], F32(0.0)).astype(BF16)
-    null_sum = lax.psum(null_part, "dp")
+    null_sum = jnp.sum(lax.all_gather(null_part, "dp"), axis=0)
 
     def whole(rows):
         every = lax.all_gather(rows, "mp", axis=0)

time: 638 us -> 612 us (0.959)
  waiting for transfers between devices: 388 us -> 334 us
  blocking collectives: 6.63 us -> 38.5 us
    all_gather x2, waiting for transfers between devices: 32.1 us -> 0.01 us  [whole(): every = lax.all_gather(rows, 'mp', axis=0)]
    all_gather x0 -> x1, blocking collectives: none -> 32.1 us  [shards(): null_sum = jnp.sum(lax.all_gather(null_part, 'dp'), axis=0)]
    psum x1 -> x0, waiting for transfers between devices: 25.2 us -> none  [shards(): null_sum = lax.psum(null_part, 'dp')]
    unnamed x69 -> x79, local copies, waits for them, and re-layouts: 17.3 us -> 16.4 us
  transfers between devices with their start and end apart: 23 -> 22, of which waited for: 16 -> 13; matrix products, arithmetic and copies ran while one was open for 24% -> 25% of each run, Pallas kernels for 0% -> 0%
where the time goes in v1:
time: 612 us; the launch traced here: 602 us
  waiting for transfers between devices  334 us (55%)
  matrix products  73.9 us (12%)
  local copies, waits for them, and re-layouts  48.3 us (8%)
  other arithmetic  47.7 us (8%)
  starting transfers between devices  43.9 us (7%)
  blocking collectives  38.5 us (6%)
  between operations  16 us (3%)
    ppermute x12, waiting for transfers between devices, swap(): return lax.ppermute(values, axis, [(i, i ^ bit) for i in range(size)])  160 us
    all_gather x2, waiting for transfers between devices, gather(): lax.all_gather(rows, 'dp', axis=0, tiled=True, axis_index_groups=lines)  104 us
    dot_general x16, matrix products, dot(): lax.dot_general(left, right, (dims, ((), ())), preferred_element_type=F32)  73.9 us
    all_to_all x1, waiting for transfers between devices, shards(): lax.all_to_all(g_down.astype(BF16).reshape(f, dp, d_rows).transpose(1, 0,...  43.5 us
    all_gather x1, blocking collectives, shards(): null_sum = jnp.sum(lax.all_gather(null_part, 'dp'), axis=0)  32.1 us
    unnamed x79, local copies, waits for them, and re-layouts  16.4 us
    all_to_all x2, waiting for transfers between devices, scatter(): lax.all_to_all(total.astype(BF16).reshape(per_line, -1, width), 'dp', 0,...  15 us
    add x2, other arithmetic, scatter(): total = product(slice(0, half)) + sent.astype(F32)  14.9 us
  transfers between devices with their start and end apart: 22, of which 13 were waited for; matrix products, arithmetic and copies ran while one was open for 25% of the time, Pallas kernels for 0%

profile of v1, /device:TPU:0, one launch (start us, length us, event | category | flops | bytes accessed | tf_op | source)
XLA Modules:
  0.0 602.0 jit_solution(2968229161004220025)
XLA Ops:
  13.5 7.3 %all-to-all-start.1 = ((bf16[8,384,384]{2,1,0:T(8,128)(2,1)}), bf16[8,384,384]{2,1,0:T(8,128)(2,1)S(1)}, u32[]{:S(2)}, u32[]{:S(2)}) async-start(bf16[8,384,384]{2,1,0:T(8,128)(2,1)} %bitcast.117), calls=%async_computation.1 | async-start | bytes 4718592 | tf_op jit(solution)/shard_map/all_to_all | solution.py:51
  22.8 68.6 %all-gather.6.cloned.1.call-done = bf16[256,3072]{1,0:T(8,128)(2,1)} async-done(((bf16[64,3072]{1,0:T(8,128)(2,1)}), bf16[256,3072]{1,0:T(8,128)(2,1)}) %all-gather.6.cloned.1.call-update) | async-done | bytes 1572880 | tf_op jit(solution)/shard_map/all_gather | solution.py:79
  92.9 35.0 %all-gather.10.cloned.1.call-done = bf16[256,3072]{1,0:T(8,128)(2,1)} async-done(((bf16[64,3072]{1,0:T(8,128)(2,1)}), bf16[256,3072]{1,0:T(8,128)(2,1)}) %all-gather.10.cloned.1.call-update) | async-done | bytes 1572880 | tf_op jit(solution)/shard_map/all_gather | solution.py:79
  143.3 20.1 %collective-permute-done.6 = bf16[256,3072]{1,0:T(8,128)(2,1)} collective-permute-done((bf16[256,3072]{1,0:T(8,128)(2,1)}, bf16[256,3072]{1,0:T(8,128)(2,1)}, u32[]{:S(2)}, u32[]{:S(2)}) %collective-permute-start.6) | collective-permute-done | bytes 1572896 | tf_op jit(solution)/shard_map/ppermute | solution.py:21
  180.6 11.9 %all-to-all-done = bf16[8,384,384]{1,2,0:T(8,128)(2,1)} async-done(((bf16[8,384,384]{1,2,0:T(8,128)(2,1)}), bf16[8,384,384]{1,2,0:T(8,128)(2,1)}, u32[]{:S(2)}, u32[]{:S(2)}) %all-to-all-start) | async-done | bytes 2359328 | tf_op jit(solution)/shard_map/all_to_all | solution.py:47
  206.0 5.6 fusion.46
  211.7 17.2 %collective-permute-done.3 = bf16[384,3072]{0,1:T(8,128)(2,1)} collective-permute-done((bf16[384,3072]{0,1:T(8,128)(2,1)S(1)}, bf16[384,3072]{0,1:T(8,128)(2,1)}, u32[]{:S(2)}, u32[]{:S(2)}) %collective-permute-start.3) | collective-permute-done | bytes 2359328 | tf_op jit(solution)/shard_map/ppermute | solution.py:21
  228.8 6.2 %fusion.47 = f32[1024,384]{1,0:T(8,128)S(1)} fusion(bf16[1024,3072]{1,0:T(8,128)(2,1)} %constant_dynamic-update-slice_fusion.3, bf16[384,3072]{0,1:T(8,128)(2,1)} %collective-permute-done.3), kind=kOutput, calls=%fused_computation.107 | convolution fusion | flops 2415919104 | bytes 10223616 | tf_op jit(solution)/shard_map/dot_general | solution.py:17
  239.4 39.6 %collective-permute-done.2 = bf16[3072,384]{1,0:T(8,128)(2,1)S(1)} collective-permute-done((bf16[3072,384]{1,0:T(8,128)(2,1)}, bf16[3072,384]{1,0:T(8,128)(2,1)S(1)}, u32[]{:S(2)}, u32[]{:S(2)}) %collective-permute-start.2) | collective-permute-done | bytes 2359328 | tf_op jit(solution)/shard_map/ppermute | solution.py:21
  311.8 29.3 %collective-permute-done.10 = bf16[3072,384]{1,0:T(8,128)(2,1)S(1)} collective-permute-done((bf16[3072,384]{1,0:T(8,128)(2,1)S(1)}, bf16[3072,384]{1,0:T(8,128)(2,1)S(1)}, u32[]{:S(2)}, u32[]{:S(2)}) %collective-permute-start.10) | collective-permute-done | bytes 2359328 | tf_op jit(solution)/shard_map/ppermute | solution.py:21
  345.9 6.9 %all-to-all-start.4 = ((bf16[8,384,384]{2,1,0:T(8,128)(2,1)}), bf16[8,384,384]{2,1,0:T(8,128)(2,1)}, u32[]{:S(2)}, u32[]{:S(2)}) async-start(bf16[8,384,384]{2,1,0:T(8,128)(2,1)} %bitcast.118), calls=%async_computation.4 | async-start | bytes 4718592 | tf_op jit(solution)/shard_map/all_to_all | solution.py:125
  352.8 6.4 %fusion.30 = f32[512,3072]{1,0:T(8,128)} fusion(bf16[3072,384]{1,0:T(8,128)(2,1)} %copy-done.2, bf16[1024,384]{1,0:T(8,128)(2,1)S(1)} %copy-done.15), kind=kOutput, calls=%fused_computation.66 | convolution fusion | flops 1207959552 | bytes 9043968 | tf_op jit(solution)/shard_map/dot_general | solution.py:17
  359.2 8.1 %convert_add_fusion = f32[512,3072]{1,0:T(8,128)} fusion(bf16[512,3072]{1,0:T(8,128)(2,1)} %collective-permute-done.8, f32[512,3072]{1,0:T(8,128)S(1)} %bitcast.87, f32[512,3072]{1,0:T(8,128)} %fusion.30), kind=kLoop, calls=%fused_computation | loop fusion | flops 4718592 | bytes 22020096 | tf_op jit(solution)/shard_map/add | solution.py:91
  375.9 6.8 %convert_add_fusion.1 = f32[512,3072]{1,0:T(8,128)} fusion(bf16[512,3072]{1,0:T(8,128)(2,1)} %collective-permute-done.4, f32[512,3072]{1,0:T(8,128)S(1)} %bitcast.85, f32[512,3072]{1,0:T(8,128)S(1)} %fusion.37), kind=kLoop, calls=%fused_computation.2 | loop fusion | flops 4718592 | bytes 22020096 | tf_op jit(solution)/shard_map/add | solution.py:91
  386.5 21.8 %collective-permute-done.9 = bf16[256,3072]{1,0:T(8,128)(2,1)} collective-permute-done((bf16[256,3072]{1,0:T(8,128)(2,1)}, bf16[256,3072]{1,0:T(8,128)(2,1)}, u32[]{:S(2)}, u32[]{:S(2)}) %collective-permute-start.9) | collective-permute-done | bytes 1572896 | tf_op jit(solution)/shard_map/ppermute | solution.py:21
  417.6 7.0 %convolution_convert_fusion = bf16[384,3072]{1,0:T(8,128)(2,1)} fusion(bf16[1024,384]{1,0:T(8,128)(2,1)S(1)} %copy-done.13, bf16[1024,3072]{1,0:T(8,128)(2,1)} %constant_dynamic-update-slice_fusion.3), kind=kOutput, calls=%fused_computation.7 | convolution fusion | flops 2417098752 | bytes 9437184 | tf_op jit(solution)/shard_map/dot_general | solution.py:17
  426.1 13.5 %collective-permute-done.5 = bf16[256,3072]{1,0:T(8,128)(2,1)} collective-permute-done((bf16[256,3072]{1,0:T(8,128)(2,1)}, bf16[256,3072]{1,0:T(8,128)(2,1)}, u32[]{:S(2)}, u32[]{:S(2)}) %collective-permute-start.5) | collective-permute-done | bytes 1572896 | tf_op jit(solution)/shard_map/ppermute | solution.py:21
  442.6 7.0 %all-to-all-done.3 = bf16[4,64,3072]{2,1,0:T(8,128)(2,1)} async-done(((bf16[4,64,3072]{2,1,0:T(8,128)(2,1)}), bf16[4,64,3072]{2,1,0:T(8,128)(2,1)}, u32[]{:S(2)}, u32[]{:S(2)}) %all-to-all-start.3) | async-done | bytes 1572896 | tf_op jit(solution)/shard_map/all_to_all | solution.py:95
  454.2 18.3 %collective-permute-done.11 = bf16[384,3072]{1,0:T(8,128)(2,1)} collective-permute-done((bf16[384,3072]{1,0:T(8,128)(2,1)}, bf16[384,3072]{1,0:T(8,128)(2,1)}, u32[]{:S(2)}, u32[]{:S(2)}) %collective-permute-start.11) | collective-permute-done | bytes 2359328 | tf_op jit(solution)/shard_map/ppermute | solution.py:21
  472.6 6.1 %add_convert_fusion.2 = bf16[384,3072]{1,0:T(8,128)(2,1)S(1)} fusion(bf16[384,3072]{1,0:T(8,128)(2,1)} %collective-permute-done.11, bf16[1024,384]{1,0:T(8,128)(2,1)S(1)} %copy-done.10, bf16[1024,3072]{1,0:T(8,128)(2,1)} %constant_dynamic-update-slice_fusion.3), kind=kOutput, calls=%fused_computation.5 | convolution fusion | flops 2419458048 | bytes 11796480 | tf_op jit(solution)/shard_map/dot_general | solution.py:17
  480.4 8.1 %all-to-all-done.2 = bf16[4,64,3072]{2,1,0:T(8,128)(2,1)S(1)} async-done(((bf16[4,64,3072]{2,1,0:T(8,128)(2,1)}), bf16[4,64,3072]{2,1,0:T(8,128)(2,1)S(1)}, u32[]{:S(2)}, u32[]{:S(2)}) %all-to-all-start.2) | async-done | bytes 1572896 | tf_op jit(solution)/shard_map/all_to_all | solution.py:95
  503.1 43.5 %all-to-all-done.5 = bf16[8,384,384]{2,1,0:T(8,128)(2,1)S(1)} async-done(((bf16[8,384,384]{2,1,0:T(8,128)(2,1)}), bf16[8,384,384]{2,1,0:T(8,128)(2,1)S(1)}, u32[]{:S(2)}, u32[]{:S(2)}) %all-to-all-start.5) | async-done | bytes 2359328 | tf_op jit(solution)/shard_map/all_to_all | solution.py:131
  550.4 32.1 %all-gather = bf16[128,3072]{1,0:T(8,128)(2,1)S(1)} all-gather(bf16[16,3072]{1,0:T(8,128)(2,1)S(1)} %fusion.42), channel_id=2, replica_groups=mesh['dp'=8,'mp'=4] {'dp'}, dimensions={0}, use_global_device_ids=true | all-gather | bytes 884736 | tf_op jit(solution)/shard_map/all_gather | solution.py:145
  582.6 6.4 %all_gather.29 = bf16[64,3072]{1,0:T(8,128)(2,1)S(1)} all-gather(bf16[16,3072]{1,0:T(8,128)(2,1)S(1)} %reduce_sum.78), channel_id=1, replica_groups=mesh['dp'=8,'mp'=4] {'mp'}, dimensions={0}, use_global_device_ids=true | all-gather | bytes 491520 | tf_op jit(solution)/shard_map/all_gather | solution.py:153
  (175 shorter events, 153.4 us)
Async XLA Ops:
  7.2 84.3 %all-gather.6.cloned.1.call-start = ((), (), s32[]{:S(2)}) async-start(), calls=%async_computation.6 | async-start | bytes 1966080 | tf_op jit(solution)/shard_map/all_gather | solution.py:79
  13.5 120.1 %all-to-all-start.1 = ((bf16[8,384,384]{2,1,0:T(8,128)(2,1)}), bf16[8,384,384]{2,1,0:T(8,128)(2,1)S(1)}, u32[]{:S(2)}, u32[]{:S(2)}) async-start(bf16[8,384,384]{2,1,0:T(8,128)(2,1)} %bitcast.117), calls=%async_computation.1 | async-start | bytes 4718592 | tf_op jit(solution)/shard_map/all_to_all | solution.py:51
  20.9 107.0 %all-gather.10.cloned.1.call-start = ((), (), s32[]{:S(2)}) async-start(), calls=%async_computation.8 | async-start | bytes 1966080 | tf_op jit(solution)/shard_map/all_gather | solution.py:79
  21.9 111.7 %copy-start.11 = (bf16[1,64,3072]{2,1,0:T(8,128)(2,1)}, bf16[1,64,3072]{2,1,0:T(8,128)(2,1)S(1)}, u32[]{:S(2)}) copy-start(bf16[1,64,3072]{2,1,0:T(8,128)(2,1)S(1)} %slice.82) | copy-start | bytes 1179652
  91.4 48.0 %collective-permute-start = (bf16[256,3072]{1,0:T(8,128)(2,1)}, bf16[256,3072]{1,0:T(8,128)(2,1)}, u32[]{:S(2)}, u32[]{:S(2)}) collective-permute-start(bf16[256,3072]{1,0:T(8,128)(2,1)} %all-gather.6.cloned.1.call-done), channel_id=1, source_target_pairs={{0,2},{1,3},{2,0},{3,1},{4,6},{5,7},{6,4},{7,5},{8,10},{9,11},{10,... | collective-permute-start | bytes 4718600 | tf_op jit(solution)/shard_map/ppermute | solution.py:21
  127.9 35.6 %collective-permute-start.6 = (bf16[256,3072]{1,0:T(8,128)(2,1)}, bf16[256,3072]{1,0:T(8,128)(2,1)}, u32[]{:S(2)}, u32[]{:S(2)}) collective-permute-start(bf16[256,3072]{1,0:T(8,128)(2,1)} %all-gather.10.cloned.1.call-done), channel_id=1, source_target_pairs={{0,2},{1,3},{2,0},{3,1},{4,6},{5,7},{6,4},{7,5},{8,10},{9,11},{10,... | collective-permute-start | bytes 4718600 | tf_op jit(solution)/shard_map/ppermute | solution.py:21
  135.1 57.4 %all-to-all-start = ((bf16[8,384,384]{1,2,0:T(8,128)(2,1)}), bf16[8,384,384]{1,2,0:T(8,128)(2,1)}, u32[]{:S(2)}, u32[]{:S(2)}) async-start(bf16[8,384,384]{1,2,0:T(8,128)(2,1)} %bitcast.104), calls=%async_computation | async-start | bytes 4718592 | tf_op jit(solution)/shard_map/all_to_all | solution.py:47
  143.3 54.9 %collective-permute-start.1 = (bf16[512,3072]{1,0:T(8,128)(2,1)}, bf16[512,3072]{1,0:T(8,128)(2,1)}, u32[]{:S(2)}, u32[]{:S(2)}) collective-permute-start(bf16[512,3072]{1,0:T(8,128)(2,1)} %pad_maximum_fusion), channel_id=1, source_target_pairs={{0,1},{1,0},{2,3},{3,2},{4,5},{5,4},{6,7},{7,6},{8,9},{9,8},{10,11... | collective-permute-start | bytes 9437192 | tf_op jit(solution)/shard_map/ppermute | solution.py:21
  166.7 35.3 %collective-permute-start.7 = (bf16[512,3072]{1,0:T(8,128)(2,1)}, bf16[512,3072]{1,0:T(8,128)(2,1)}, u32[]{:S(2)}, u32[]{:S(2)}) collective-permute-start(bf16[512,3072]{1,0:T(8,128)(2,1)} %pad_maximum_fusion.1), channel_id=1, source_target_pairs={{0,1},{1,0},{2,3},{3,2},{4,5},{5,4},{6,7},{7,6},{8,9},{9,8},{10,11... | collective-permute-start | bytes 9437192 | tf_op jit(solution)/shard_map/ppermute | solution.py:21
  171.0 57.8 %collective-permute-start.3 = (bf16[384,3072]{0,1:T(8,128)(2,1)S(1)}, bf16[384,3072]{0,1:T(8,128)(2,1)}, u32[]{:S(2)}, u32[]{:S(2)}) collective-permute-start(bf16[384,3072]{0,1:T(8,128)(2,1)S(1)} %bitcast.88), channel_id=1, source_target_pairs={{0,4},{4,0},{8,12},{12,8},{16,20},{20,16},{24,28},{28,24},{1,5},{5... | collective-permute-start | bytes 7077896 | tf_op jit(solution)/shard_map/ppermute | solution.py:21
  196.7 82.3 %collective-permute-start.2 = (bf16[3072,384]{1,0:T(8,128)(2,1)}, bf16[3072,384]{1,0:T(8,128)(2,1)S(1)}, u32[]{:S(2)}, u32[]{:S(2)}) collective-permute-start(bf16[3072,384]{1,0:T(8,128)(2,1)} %bitcast.92), channel_id=1, source_target_pairs={{0,4},{4,0},{8,12},{12,8},{16,20},{20,16},{24,28},{28,24},{1,5},{5... | collective-permute-start | bytes 7077896 | tf_op jit(solution)/shard_map/ppermute | solution.py:21
  239.4 67.9 %copy-start.9 = (bf16[1024,384]{1,0:T(8,128)(2,1)}, bf16[1024,384]{1,0:T(8,128)(2,1)S(1)}, u32[]{:S(2)}) copy-start(bf16[1024,384]{1,0:T(8,128)(2,1)S(1)} %get-tuple-element.11) | copy-start | bytes 2359300
  287.6 53.5 %collective-permute-start.10 = (bf16[3072,384]{1,0:T(8,128)(2,1)S(1)}, bf16[3072,384]{1,0:T(8,128)(2,1)S(1)}, u32[]{:S(2)}, u32[]{:S(2)}) collective-permute-start(bf16[3072,384]{1,0:T(8,128)(2,1)S(1)} %convolution_convert_fusion.1), channel_id=1, source_target_pairs={{0,4},{4,0},{8,12},{12,8},{16,20},{20,16},{24,28},{28,24},{1,5},{5... | collective-permute-start | bytes 7077896 | tf_op jit(solution)/shard_map/ppermute | solution.py:21
  295.4 63.8 %collective-permute-start.8 = (bf16[512,3072]{1,0:T(8,128)(2,1)}, bf16[512,3072]{1,0:T(8,128)(2,1)}, u32[]{:S(2)}, u32[]{:S(2)}) collective-permute-start(bf16[512,3072]{1,0:T(8,128)(2,1)} %add_convert_fusion), channel_id=1, source_target_pairs={{0,1},{1,0},{2,3},{3,2},{4,5},{5,4},{6,7},{7,6},{8,9},{9,8},{10,11... | collective-permute-start | bytes 9437192 | tf_op jit(solution)/shard_map/ppermute | solution.py:21
  302.5 73.4 %collective-permute-start.4 = (bf16[512,3072]{1,0:T(8,128)(2,1)}, bf16[512,3072]{1,0:T(8,128)(2,1)}, u32[]{:S(2)}, u32[]{:S(2)}) collective-permute-start(bf16[512,3072]{1,0:T(8,128)(2,1)} %add_convert_fusion.1), channel_id=1, source_target_pairs={{0,1},{1,0},{2,3},{3,2},{4,5},{5,4},{6,7},{7,6},{8,9},{9,8},{10,11... | collective-permute-start | bytes 9437192 | tf_op jit(solution)/shard_map/ppermute | solution.py:21
  345.9 66.3 %all-to-all-start.4 = ((bf16[8,384,384]{2,1,0:T(8,128)(2,1)}), bf16[8,384,384]{2,1,0:T(8,128)(2,1)}, u32[]{:S(2)}, u32[]{:S(2)}) async-start(bf16[8,384,384]{2,1,0:T(8,128)(2,1)} %bitcast.118), calls=%async_computation.4 | async-start | bytes 4718592 | tf_op jit(solution)/shard_map/all_to_all | solution.py:125
  370.8 37.6 %collective-permute-start.9 = (bf16[256,3072]{1,0:T(8,128)(2,1)}, bf16[256,3072]{1,0:T(8,128)(2,1)}, u32[]{:S(2)}, u32[]{:S(2)}) collective-permute-start(bf16[256,3072]{1,0:T(8,128)(2,1)} %slice.154), channel_id=1, source_target_pairs={{0,2},{1,3},{2,0},{3,1},{4,6},{5,7},{6,4},{7,5},{8,10},{9,11},{10,... | collective-permute-start | bytes 4718600 | tf_op jit(solution)/shard_map/ppermute | solution.py:21
  385.9 53.6 %collective-permute-start.5 = (bf16[256,3072]{1,0:T(8,128)(2,1)}, bf16[256,3072]{1,0:T(8,128)(2,1)}, u32[]{:S(2)}, u32[]{:S(2)}) collective-permute-start(bf16[256,3072]{1,0:T(8,128)(2,1)} %slice.155), channel_id=1, source_target_pairs={{0,2},{1,3},{2,0},{3,1},{4,6},{5,7},{6,4},{7,5},{8,10},{9,11},{10,... | collective-permute-start | bytes 4718600 | tf_op jit(solution)/shard_map/ppermute | solution.py:21
  412.3 37.3 %all-to-all-start.3 = ((bf16[4,64,3072]{2,1,0:T(8,128)(2,1)}), bf16[4,64,3072]{2,1,0:T(8,128)(2,1)}, u32[]{:S(2)}, u32[]{:S(2)}) async-start(bf16[4,64,3072]{2,1,0:T(8,128)(2,1)} %bitcast.106), calls=%async_computation.3 | async-start | bytes 3145728 | tf_op jit(solution)/shard_map/all_to_all | solution.py:95
  424.6 47.9 %collective-permute-start.11 = (bf16[384,3072]{1,0:T(8,128)(2,1)}, bf16[384,3072]{1,0:T(8,128)(2,1)}, u32[]{:S(2)}, u32[]{:S(2)}) collective-permute-start(bf16[384,3072]{1,0:T(8,128)(2,1)} %convolution_convert_fusion), channel_id=1, source_target_pairs={{0,4},{4,0},{8,12},{12,8},{16,20},{20,16},{24,28},{28,24},{1,5},{5... | collective-permute-start | bytes 7077896 | tf_op jit(solution)/shard_map/ppermute | solution.py:21
  449.6 38.9 %all-to-all-start.2 = ((bf16[4,64,3072]{2,1,0:T(8,128)(2,1)}), bf16[4,64,3072]{2,1,0:T(8,128)(2,1)S(1)}, u32[]{:S(2)}, u32[]{:S(2)}) async-start(bf16[4,64,3072]{2,1,0:T(8,128)(2,1)} %bitcast.107), calls=%async_computation.2 | async-start | bytes 3145728 | tf_op jit(solution)/shard_map/all_to_all | solution.py:95
  489.6 57.0 %all-to-all-start.5 = ((bf16[8,384,384]{2,1,0:T(8,128)(2,1)}), bf16[8,384,384]{2,1,0:T(8,128)(2,1)S(1)}, u32[]{:S(2)}, u32[]{:S(2)}) async-start(bf16[8,384,384]{2,1,0:T(8,128)(2,1)} %bitcast.103), calls=%async_computation.5 | async-start | bytes 4718592 | tf_op jit(solution)/shard_map/all_to_all | solution.py:131
  493.3 96.7 %all-gather.8.cloned.1.call-start = ((), (), s32[]{:S(2)}) async-start(), calls=%async_computation.7 | async-start | bytes 1966080 | tf_op jit(solution)/shard_map/all_gather | solution.py:148
  498.1 94.5 %all-gather.12.cloned.1.call-start = ((), (), s32[]{:S(2)}) async-start(), calls=%async_computation.9 | async-start | bytes 1966080 | tf_op jit(solution)/shard_map/all_gather | solution.py:148
  (40 other events, 483.3 us)
Sparse Core Ops, SparseCore 0:
  13.6 77.7 all-gather.5
  93.6 34.2 all-gather.9
  498.2 20.9 all-gather.7
  520.7 19.6 all-gather.11
